TPU v7x, 32 devices: a whole 2x2x4 slice. The times are simulated.
32 devices in a mesh: parts: 2 (over x), frame: 2 (over core), tile: 8 (over z, y).
Axes of the slice: x: 2, y: 2, z: 4, core: 2. Of those that a mesh axis runs over, the one named last changes fastest.
Arguments:
- decoded_refs: bfloat16 [64, 96, 64, 256], P(('parts', 'frame'), None, 'tile'), parts along dimension 0, may hold values from -6 to 6
- current_frames: bfloat16 [16, 96, 64, 256], P(('parts', 'frame'), None, 'tile'), parts along dimension 0, may hold values from -6 to 6
- ref_pairs: int32 [16, 2], P('parts'), parts along dimension 0, may hold values from 0 to 31
- ref_slots: int32 [64], P('parts'), parts along dimension 0, may hold values from 0 to 31, each once
- frame_numbers: int32 [16], P('parts'), parts along dimension 0, may hold values from 0 to 31
- rate_weights: float32 [64], P('parts'), parts along dimension 0, may hold values from 0.5 to 4
- join_kernel: bfloat16 [3, 3, 96, 288], replicated, may hold values from -0.125 to 0.125
- out_kernel: bfloat16 [3, 3, 96, 96], replicated, may hold values from -0.21875 to 0.21875
Outputs:
- reconstruction: bfloat16 [16, 96, 64, 256], P(('parts', 'frame'), None, 'tile'), parts along dimension 0
- join_grad: float32 [6, 3, 96, 288], P('parts'), parts along dimension 0
- output_grad: float32 [6, 3, 96, 96], P('parts'), parts along dimension 0
There are 2 independent parts, one for each index of `parts`. A program takes and returns all parts, laid end to end along the dimension named above; an argument that names none is the same for every part. Nothing has to cross between parts.
Inputs may be any that keep to these rules, and one draw needn't show every extreme that they name: `ref_pairs`: each B-frame names two decoded frames, possibly the same one. `ref_slots`: each slot holds exactly one decoded frame.
All inputs are finite; a program needn't handle non-finite values.
Results may differ from a plain program's by a relative error of at most 0.005.
Values may be sent and summed in bfloat16 or wider, within the bound.
No kernel may reach another device: no remote copies, remote signals or barrier semaphores. Data moves between devices by JAX's collectives and lax.ppermute only.
A program may use at most 128 MiB of HBM per device.

v0:
```python
import jax
import jax.numpy as jnp
from jax import lax
from jax.sharding import PartitionSpec as P


def partner(array, axis, stride):
    return lax.ppermute(array, axis, [(i, i ^ 1 << stride) for i in range(lax.axis_size(axis))])


def with_halo(cells, sides, width):
    for axis, dim in sides:
        count = lax.axis_size(axis)
        ends = count - 1
        head = lax.slice_in_dim(cells, 0, width, axis=dim)
        tail = lax.slice_in_dim(cells, cells.shape[dim] - width, cells.shape[dim], axis=dim)
        cells = jnp.concatenate(
            [
                lax.ppermute(tail, axis, [(i, (i + 1) % count) for i in range(ends)]),
                cells,
                lax.ppermute(head, axis, [((i + 1) % count, i) for i in range(ends)]),
            ],
            axis=dim,
        )
    return cells


def pad_cols(field):
    return jnp.pad(field, ((0, 0), (0, 0), (0, 0), (1, 1)))


def apply_taps(padded, kernel, row_count, col_count):
    running = None
    for row_tap in range(3):
        for col_tap in range(3):
            window = padded[:, :, row_tap : row_tap + row_count, col_tap : col_tap + col_count]
            partial_sum = jnp.einsum(
                "oi,bihw->bohw",
                kernel[row_tap, col_tap],
                window,
                preferred_element_type=jnp.float32,
            )
            running = partial_sum if running is None else running + partial_sum
    return running


def tap_grads(upstream, padded, row_count, col_count):
    pieces = []
    for row_tap in range(3):
        for col_tap in range(3):
            window = padded[:, :, row_tap : row_tap + row_count, col_tap : col_tap + col_count]
            pieces.append(
                jnp.einsum("bohw,bihw->oi", upstream, window, preferred_element_type=jnp.float32)
            )
    stacked = jnp.stack(pieces)
    return stacked.reshape((3, 3) + stacked.shape[1:])


def transpose_taps(padded, kernel, row_count, col_count):
    running = None
    for row_tap in range(3):
        for col_tap in range(3):
            window = padded[
                :, :, 2 - row_tap : 2 - row_tap + row_count, 2 - col_tap : 2 - col_tap + col_count
            ]
            partial_sum = jnp.einsum(
                "oi,bohw->bihw",
                kernel[row_tap, col_tap],
                window,
                preferred_element_type=jnp.float32,
            )
            running = partial_sum if running is None else running + partial_sum
    return running


def on_device(
    decoded_refs,
    current_frames,
    ref_pairs,
    ref_slots,
    frame_numbers,
    rate_weights,
    join_kernel,
    out_kernel,
):
    local_refs = decoded_refs.shape[0]
    local_frames, channels, tile_rows, col_count = current_frames.shape
    group = lax.axis_index("frame")
    frame_range = jnp.arange(ref_slots.shape[0], dtype=jnp.int32)

    def pair_slots(which):
        pairs = lax.dynamic_slice_in_dim(ref_pairs, which * local_frames, local_frames, 0)
        return jnp.sum(jnp.where(pairs[:, :, None] == frame_range, ref_slots, 0), axis=-1).reshape(
            -1
        )

    mine = pair_slots(group)
    other = pair_slots(1 - group) - group * local_refs
    other_held = (other >= 0) & (other < local_refs)
    outgoing = jnp.take(decoded_refs, jnp.clip(other, 0, local_refs - 1), axis=0)
    outgoing = jnp.where(other_held[:, None, None, None], outgoing, jnp.zeros((), jnp.bfloat16))
    incoming = partner(outgoing, "frame", 0)
    mine_local = mine - group * local_refs
    mine_held = (mine_local >= 0) & (mine_local < local_refs)
    own_tiles = jnp.take(decoded_refs, jnp.clip(mine_local, 0, local_refs - 1), axis=0)
    picked = jnp.where(mine_held[:, None, None, None], own_tiles, incoming)
    picked = picked.reshape(local_frames, 2 * channels, tile_rows, col_count)
    stacked = jnp.concatenate([picked, current_frames], axis=1)
    height = tile_rows * lax.axis_size("tile")
    stacked_pad = pad_cols(with_halo(stacked, (("tile", 2),), 1))
    preact = apply_taps(stacked_pad, join_kernel, tile_rows, col_count)
    hidden = jax.nn.silu(preact).astype(jnp.bfloat16)
    hidden_pad = pad_cols(with_halo(hidden, (("tile", 2),), 1))
    recon = apply_taps(hidden_pad, out_kernel, tile_rows, col_count)
    frames_here = lax.dynamic_slice_in_dim(frame_numbers, group * local_frames, local_frames, 0)
    gop_range = jnp.arange(rate_weights.shape[0], dtype=jnp.int32)
    weight_here = jnp.sum(jnp.where(frames_here[:, None] == gop_range, rate_weights, 0.0), axis=-1)
    residual = (
        2.0
        * weight_here[:, None, None, None]
        * (recon - current_frames.astype(jnp.float32))
        / (height * col_count)
    ).astype(jnp.bfloat16)
    output_part = tap_grads(residual, hidden_pad, tile_rows, col_count)
    residual_pad = pad_cols(with_halo(residual, (("tile", 2),), 1))
    hidden_grad = transpose_taps(residual_pad, out_kernel, tile_rows, col_count)
    sigma = jax.nn.sigmoid(preact)
    preact_grad = (hidden_grad * (sigma * (1.0 + preact * (1.0 - sigma)))).astype(jnp.bfloat16)
    join_part = tap_grads(preact_grad, stacked_pad, tile_rows, col_count)
    join_total, output_total = lax.psum((join_part, output_part), ("frame", "tile"))
    return (recon.astype(jnp.bfloat16), join_total, output_total)


def solution(mesh):
    placed = (
        P(("parts", "frame"), None, "tile", None),
        P(("parts", "frame"), None, "tile", None),
        P("parts", None),
        P("parts"),
        P("parts"),
        P("parts"),
        P(),
        P(),
    )
    return jax.shard_map(
        on_device,
        mesh=mesh,
        in_specs=placed,
        out_specs=(
            P(("parts", "frame"), None, "tile", None),
            P("parts", None, None, None),
            P("parts", None, None, None),
        ),
        check_vma=False,
    )
```

profile of v0, /device:TPU:0, one launch (start us, length us, event | category | flops | bytes accessed | tf_op | source)
XLA Modules:
  0.0 316.3 jit_solution(6652373692335212695)
XLA Ops:
  7.2 0.8 constant_dynamic-slice_fusion
  8.0 0.9 select_reduce_fusion.1
  9.5 3.5 %gather_fusion.1 = bf16[8,96,8,256]{3,2,1,0:T(8,128)(2,1)S(1)} fusion(bf16[16,96,8,256]{3,2,1,0:T(8,128)(2,1)} %param.10, s32[1024]{0:T(1024)S(1)} %pad_clamp_fusion), kind=kCustom, calls=%fused_computation.1.clone | custom fusion | bytes 6291488 | tf_op jit(solution)/shard_map/jit(_take)/gather | solution.py:100
  13.1 2.1 select_select_fusion
  15.9 3.5 %gather_fusion = bf16[8,96,8,256]{3,2,1,0:T(8,128)(2,1)S(1)} fusion(bf16[16,96,8,256]{3,2,1,0:T(8,128)(2,1)} %param.10, s32[1024]{0:T(1024)S(1)} %pad_clamp_fusion.1), kind=kCustom, calls=%fused_computation.clone | custom fusion | bytes 6291488 | tf_op jit(solution)/shard_map/jit(_take)/gather | solution.py:105
  19.7 1.6 collective-permute-done
  21.3 2.3 select_select_fusion.1
  25.4 4.8 %collective-permute-start.1 = (bf16[4,288,1,256]{3,1,2,0:T(8,128)(2,1)S(1)}, bf16[4,288,1,256]{3,1,2,0:T(8,128)(2,1)S(1)}, u32[]{:S(2)}, u32[]{:S(2)}) collective-permute-start(bf16[4,288,1,256]{3,1,2,0:T(8,128)(2,1)S(1)} %get-tuple-element.17), channel_id=1, source_target_pairs={{0,1},{1,2},{2,3},{3,4},{4,5},{5,6},{6,7},{8,9},{9,10},{10,11},{11... | collective-permute-start | bytes 1769480 | tf_op jit(solution)/shard_map/ppermute | solution.py:19
  30.3 1.6 collective-permute-start.2
  31.9 3.0 fusion.184
  34.9 20.8 %collective-permute-done.1 = bf16[4,288,1,256]{3,1,2,0:T(8,128)(2,1)S(1)} collective-permute-done((bf16[4,288,1,256]{3,1,2,0:T(8,128)(2,1)S(1)}, bf16[4,288,1,256]{3,1,2,0:T(8,128)(2,1)S(1)}, u32[]{:S(2)}, u32[]{:S(2)}) %collective-permute-start.1) | collective-permute-done | bytes 589856 | tf_op jit(solution)/shard_map/ppermute | solution.py:19
  55.8 5.9 %fusion.5 = bf16[4,288,10,258]{3,1,2,0:T(8,128)(2,1)S(1)} fusion(bf16[4,288,1,256]{3,1,2,0:T(8,128)(2,1)S(1)} %collective-permute-done.2, bf16[4,288,8,256]{3,1,2,0:T(8,128)(2,1)S(1)} %copy_dynamic-update-slice_fusion.1, bf16[4,288,1,256]{3,1,2,0:T(8,128)(2,1)S(1)} %collective-permute-done.1), kind=kLoop, calls=%fused_computation.9 | loop fusion | flops 35665920 | bytes 11842560 | tf_op jit(solution)/shard_map/concatenate | solution.py:17
  61.7 3.0 fusion.13
  64.7 3.3 %fusion.17 = f32[4,8,256,96]{2,3,1,0:T(8,128)} fusion(bf16[4,288,10,258]{3,1,2,0:T(8,128)(2,1)S(1)} %fusion.5, bf16[3,3,96,288]{3,2,1,0:T(8,128)(2,1)S(1)} %copy-done.8), kind=kOutput, calls=%fused_computation.25 | convolution fusion | flops 452984832 | bytes 7938048 | tf_op jit(solution)/shard_map/oi,bihw->bohw/dot_general | solution.py:37
  68.0 3.0 fusion.21
  71.0 3.3 %fusion.25 = f32[4,8,256,96]{2,3,1,0:T(8,128)} fusion(bf16[4,288,10,258]{3,1,2,0:T(8,128)(2,1)S(1)} %fusion.5, bf16[3,3,96,288]{3,2,1,0:T(8,128)(2,1)S(1)} %copy-done.8), kind=kOutput, calls=%fused_computation.33 | convolution fusion | flops 452984832 | bytes 7938048 | tf_op jit(solution)/shard_map/oi,bihw->bohw/dot_general | solution.py:37
  74.3 3.0 fusion.29
  77.2 3.0 fusion.44
  80.3 3.0 fusion.42
  83.2 11.2 %fusion.38 = (bf16[4,96,8,256]{3,1,2,0:T(8,128)(2,1)}, f32[4,8,256,96]{2,3,1,0:T(8,128)}) fusion(bf16[4,288,10,258]{3,1,2,0:T(8,128)(2,1)S(1)} %fusion.5, bf16[3,3,96,288]{3,2,1,0:T(8,128)(2,1)} %param.16, f32[4,8,256,96]{2,3,1,0:T(8,128)} %fusion.44, f32[4,8,256,96]{2,3,1,0:T(8,128)} %fusion.13, f32[4,8,256,96]{2,3,1,0:T(8,128)} %fusion.17, ...), kind=kOutput, calls=%fused_computation.52 | convolution fusion | flops 463208448 | bytes 34676736 | tf_op jit(solution)/shard_map/oi,bihw->bohw/dot_general | solution.py:37
  94.4 1.2 fusion.249
  95.6 4.4 %collective-permute-start.3 = (bf16[4,96,1,256]{3,1,2,0:T(8,128)(2,1)S(1)}, bf16[4,96,1,256]{3,1,2,0:T(8,128)(2,1)S(1)}, u32[]{:S(2)}, u32[]{:S(2)}) collective-permute-start(bf16[4,96,1,256]{3,1,2,0:T(8,128)(2,1)S(1)} %get-tuple-element.21), channel_id=1, source_target_pairs={{0,1},{1,2},{2,3},{3,4},{4,5},{5,6},{6,7},{8,9},{9,10},{10,11},{11... | collective-permute-start | bytes 589832 | tf_op jit(solution)/shard_map/ppermute | solution.py:19
  100.0 1.8 collective-permute-start.4
  101.8 3.7 %fusion.209 = f32[4,8,256,96]{2,3,1,0:T(8,128)} fusion(bf16[4,96,8,256]{3,1,2,0:T(8,128)(2,1)} %get-tuple-element.25, bf16[3,3,96,96]{3,2,1,0:T(8,128)(2,1)S(1)} %copy-done.4), kind=kOutput, calls=%fused_computation.183 | convolution fusion | flops 150994944 | bytes 4743168 | tf_op jit(solution)/shard_map/oi,bihw->bohw/dot_general | solution.py:37
  105.5 3.6 %collective-permute-done.4 = bf16[4,96,1,256]{3,1,2,0:T(8,128)(2,1)S(1)} collective-permute-done((bf16[4,96,1,256]{3,1,2,0:T(8,128)(2,1)S(1)}, bf16[4,96,1,256]{3,1,2,0:T(8,128)(2,1)S(1)}, u32[]{:S(2)}, u32[]{:S(2)}) %collective-permute-start.4) | collective-permute-done | bytes 196640 | tf_op jit(solution)/shard_map/ppermute | solution.py:21
  109.1 2.0 select_maximum_fusion.2
  111.1 2.2 fusion.76
  113.3 2.4 fusion.80
  115.7 2.2 fusion.84
  117.9 2.3 fusion.88
  120.2 2.2 fusion.92
  122.5 2.2 fusion.175
  124.7 2.3 fusion.174
  126.9 12.3 %bitcast_convert_fusion = (bf16[4,96,8,256]{3,1,2,0:T(8,128)(2,1)}, f32[4,8,256,96]{2,3,1,0:T(8,128)}) fusion(bf16[4,96,10,258]{3,1,2,0:T(8,128)(2,1)S(1)} %select_maximum_fusion.2, bf16[3,3,96,96]{3,2,1,0:T(8,128)(2,1)S(1)} %copy-done.4, f32[4,8,256,96]{2,3,1,0:T(8,128)} %fusion.175, f32[4,8,256,96]{2,3,1,0:T(8,128)} %fusion.76, ...), kind=kOutput, calls=%fused_computation.42 | convolution fusion | flops 158072832 | bytes 31481856 | tf_op jit(solution)/shard_map/oi,bihw->bohw/dot_general | solution.py:37
  139.2 2.6 fusion.34
  142.5 2.3 fusion.207
  144.8 1.3 collective-permute-start.6
  146.0 5.4 %collective-permute-start.5 = (bf16[4,96,1,256]{3,1,2,0:T(8,128)(2,1)S(1)}, bf16[4,96,1,256]{3,1,2,0:T(8,128)(2,1)S(1)}, u32[]{:S(2)}, u32[]{:S(2)}) collective-permute-start(bf16[4,96,1,256]{3,1,2,0:T(8,128)(2,1)S(1)} %get-tuple-element.20), channel_id=1, source_target_pairs={{0,1},{1,2},{2,3},{3,4},{4,5},{5,6},{6,7},{8,9},{9,10},{10,11},{11... | collective-permute-start | bytes 589832 | tf_op jit(solution)/shard_map/ppermute | solution.py:19
  153.9 0.8 fusion.156
  155.8 0.8 fusion.168
  156.6 2.0 collective-permute-done.5
  158.6 2.0 select_maximum_fusion
  160.6 2.5 fusion.58
  163.1 2.3 fusion.60
  165.4 2.4 fusion.62
  167.8 2.3 fusion.64
  170.1 2.5 fusion.66
  172.6 2.3 fusion.50
  174.8 2.3 fusion.46
  177.1 10.6 %fusion.31 = bf16[4,96,8,256]{3,1,2,0:T(8,128)(2,1)S(1)} fusion(f32[4,8,256,96]{2,3,1,0:T(8,128)} %get-tuple-element.26, f32[4,8,256,96]{2,3,1,0:T(8,128)} %fusion.50, f32[4,8,256,96]{2,3,1,0:T(8,128)} %fusion.58, f32[4,8,256,96]{2,3,1,0:T(8,128)} %fusion.60, f32[4,8,256,96]{2,3,1,0:T(8,128)} %fusion.207, f32[4,8,256,96]{2,3,1,0:T(8,128)} %fusion.62, ...), kind=kOutput, calls=%fused_computation.40 | convolution fusion | flops 164364288 | bytes 31481856 | tf_op jit(solution)/shard_map/oi,bohw->bihw/dot_general | solution.py:66
  187.7 1.8 fusion.101
  189.5 1.8 fusion.97
  191.3 2.3 fusion.107
  193.6 1.8 fusion.113
  195.3 1.8 fusion.134
  197.1 2.3 fusion.119
  199.4 1.8 fusion.125
  201.1 1.8 fusion.95
  202.9 2.3 fusion.131
  205.2 1.1 copy-done.3
  206.3 3.4 %copy.56 = bf16[4,96,8,256]{3,2,1,0:T(8,128)(2,1)} copy(bf16[4,96,8,256]{3,1,2,0:T(8,128)(2,1)} %get-tuple-element.27) | data formatting | bytes 3145728
  209.7 95.2 %all-reduce.6.cloned.1.call-done = (f32[3,3,96,288]{3,2,1,0:T(8,128)}, f32[3,3,96,96]{3,2,1,0:T(8,128)}) async-done(((f32[3,3,96,288]{3,2,1,0:T(8,128)}, f32[3,3,96,96]{3,2,1,0:T(8,128)}), (f32[3,3,96,288]{3,2,1,0:T(8,128)}, f32[3,3,96,96]{3,2,1,0:T(8,128)})) %all-reduce.6.cloned.1.call-update) | async-done | bytes 1327120 | tf_op jit(solution)/shard_map/psum | solution.py:130
  304.9 2.5 copy.133
  307.4 1.8 copy.134
  (57 shorter events, 7.6 us)
Async XLA Ops:
  7.2 297.8 %all-reduce.6.cloned.1.call-start = ((), (), s32[]{:S(2)}) async-start(), calls=%async_computation | async-start | bytes 3538944 | tf_op jit(solution)/shard_map/psum | solution.py:130
  13.1 2.6 copy-start.9
  15.2 6.1 %collective-permute-start = (bf16[8,96,8,256]{3,2,1,0:T(8,128)(2,1)}, bf16[8,96,8,256]{3,2,1,0:T(8,128)(2,1)}, u32[]{:S(2)}, u32[]{:S(2)}) collective-permute-start(bf16[8,96,8,256]{3,2,1,0:T(8,128)(2,1)} %select_select_fusion), channel_id=1, source_target_pairs={{0,8},{8,0},{1,9},{9,1},{2,10},{10,2},{3,11},{11,3},{4,12},{12,4},... | collective-permute-start | bytes 9437192 | tf_op jit(solution)/shard_map/ppermute | solution.py:8
  15.9 3.6 %copy-start.10 = (f32[32]{0:T(128)S(1)}, f32[32]{0:T(128)}, u32[]{:S(2)}) copy-start(f32[32]{0:T(128)} %param.15) | copy-start | bytes 388
  23.6 1.4 copy-start.1
  25.0 6.9 %copy-start.8 = (bf16[3,3,96,288]{3,2,1,0:T(8,128)(2,1)S(1)}, bf16[3,3,96,288]{3,2,1,0:T(8,128)(2,1)}, u32[]{:S(2)}) copy-start(bf16[3,3,96,288]{3,2,1,0:T(8,128)(2,1)} %param.16) | copy-start | bytes 1492996
  25.4 30.3 %collective-permute-start.1 = (bf16[4,288,1,256]{3,1,2,0:T(8,128)(2,1)S(1)}, bf16[4,288,1,256]{3,1,2,0:T(8,128)(2,1)S(1)}, u32[]{:S(2)}, u32[]{:S(2)}) collective-permute-start(bf16[4,288,1,256]{3,1,2,0:T(8,128)(2,1)S(1)} %get-tuple-element.17), channel_id=1, source_target_pairs={{0,1},{1,2},{2,3},{3,4},{4,5},{5,6},{6,7},{8,9},{9,10},{10,11},{11... | collective-permute-start | bytes 1769480 | tf_op jit(solution)/shard_map/ppermute | solution.py:19
  30.3 25.5 %collective-permute-start.2 = (bf16[4,288,1,256]{3,1,2,0:T(8,128)(2,1)S(1)}, bf16[4,288,1,256]{3,1,2,0:T(8,128)(2,1)S(1)}, u32[]{:S(2)}, u32[]{:S(2)}) collective-permute-start(bf16[4,288,1,256]{3,1,2,0:T(8,128)(2,1)S(1)} %get-tuple-element.18), channel_id=1, source_target_pairs={{1,0},{2,1},{3,2},{4,3},{5,4},{6,5},{7,6},{9,8},{10,9},{11,10},{12... | collective-permute-start | bytes 1769480 | tf_op jit(solution)/shard_map/ppermute | solution.py:21
  55.7 24.5 %copy-start.5 = (bf16[4,288,1,256]{3,1,2,0:T(8,128)(2,1)}, bf16[4,288,1,256]{3,1,2,0:T(8,128)(2,1)S(1)}, u32[]{:S(2)}) copy-start(bf16[4,288,1,256]{3,1,2,0:T(8,128)(2,1)S(1)} %collective-permute-done.1) | copy-start | bytes 1769476
  83.2 18.6 %copy-start.4 = (bf16[3,3,96,96]{3,2,1,0:T(8,128)(2,1)S(1)}, bf16[3,3,96,96]{3,2,1,0:T(8,128)(2,1)}, u32[]{:S(2)}) copy-start(bf16[3,3,96,96]{3,2,1,0:T(8,128)(2,1)} %param.17) | copy-start | bytes 497668
  94.4 14.7 %copy-start = (bf16[4,96,8,256]{3,1,2,0:T(8,128)(2,1)S(1)}, bf16[4,96,8,256]{3,1,2,0:T(8,128)(2,1)}, u32[]{:S(2)}) copy-start(bf16[4,96,8,256]{3,1,2,0:T(8,128)(2,1)} %get-tuple-element.25) | copy-start | bytes 4718596
  95.6 9.9 %collective-permute-start.3 = (bf16[4,96,1,256]{3,1,2,0:T(8,128)(2,1)S(1)}, bf16[4,96,1,256]{3,1,2,0:T(8,128)(2,1)S(1)}, u32[]{:S(2)}, u32[]{:S(2)}) collective-permute-start(bf16[4,96,1,256]{3,1,2,0:T(8,128)(2,1)S(1)} %get-tuple-element.21), channel_id=1, source_target_pairs={{0,1},{1,2},{2,3},{3,4},{4,5},{5,6},{6,7},{8,9},{9,10},{10,11},{11... | collective-permute-start | bytes 589832 | tf_op jit(solution)/shard_map/ppermute | solution.py:19
  100.0 9.1 %collective-permute-start.4 = (bf16[4,96,1,256]{3,1,2,0:T(8,128)(2,1)S(1)}, bf16[4,96,1,256]{3,1,2,0:T(8,128)(2,1)S(1)}, u32[]{:S(2)}, u32[]{:S(2)}) collective-permute-start(bf16[4,96,1,256]{3,1,2,0:T(8,128)(2,1)S(1)} %get-tuple-element.22), channel_id=1, source_target_pairs={{1,0},{2,1},{3,2},{4,3},{5,4},{6,5},{7,6},{9,8},{10,9},{11,10},{12... | collective-permute-start | bytes 589832 | tf_op jit(solution)/shard_map/ppermute | solution.py:21
  126.9 12.3 %copy-start.2 = (bf16[4,96,8,256]{3,2,1,0:T(8,128)(2,1)S(1)}, bf16[4,96,8,256]{3,2,1,0:T(8,128)(2,1)}, u32[]{:S(2)}) copy-start(bf16[4,96,8,256]{3,2,1,0:T(8,128)(2,1)} %param.11) | copy-start | bytes 4718596
  144.8 11.9 %collective-permute-start.6 = (bf16[4,96,1,256]{3,1,2,0:T(8,128)(2,1)S(1)}, bf16[4,96,1,256]{3,1,2,0:T(8,128)(2,1)S(1)}, u32[]{:S(2)}, u32[]{:S(2)}) collective-permute-start(bf16[4,96,1,256]{3,1,2,0:T(8,128)(2,1)S(1)} %get-tuple-element.19), channel_id=1, source_target_pairs={{1,0},{2,1},{3,2},{4,3},{5,4},{6,5},{7,6},{9,8},{10,9},{11,10},{12... | collective-permute-start | bytes 589832 | tf_op jit(solution)/shard_map/ppermute | solution.py:21
  146.0 12.6 %collective-permute-start.5 = (bf16[4,96,1,256]{3,1,2,0:T(8,128)(2,1)S(1)}, bf16[4,96,1,256]{3,1,2,0:T(8,128)(2,1)S(1)}, u32[]{:S(2)}, u32[]{:S(2)}) collective-permute-start(bf16[4,96,1,256]{3,1,2,0:T(8,128)(2,1)S(1)} %get-tuple-element.20), channel_id=1, source_target_pairs={{0,1},{1,2},{2,3},{3,4},{4,5},{5,6},{6,7},{8,9},{9,10},{10,11},{11... | collective-permute-start | bytes 589832 | tf_op jit(solution)/shard_map/ppermute | solution.py:19
  156.6 6.4 %copy-start.7 = (f32[9,96,96]{2,1,0:T(8,128)}, f32[9,96,96]{2,1,0:T(8,128)S(1)}, u32[]{:S(2)}) copy-start(f32[9,96,96]{2,1,0:T(8,128)S(1)} %fusion.168) | copy-start | bytes 995332
  187.7 1.8 copy-start.6
  205.2 1.1 copy-start.3
Sparse Core Ops, SparseCore 0:
  206.4 98.4 all-reduce.5
where the time goes:
time: 320 us; the launch traced here: 316 us
  waiting for transfers between devices  123 us (38%)
  matrix products  120 us (38%)
  local copies, waits for them, and re-layouts  20.6 us (6%)
  starting transfers between devices  19.8 us (6%)
  other arithmetic  18 us (6%)
  between operations  14.7 us (5%)
    psum x1, waiting for transfers between devices, on_device(): lax.psum((join_part, output_part), ('frame', 'tile'))  95.2 us
    dot_general x18, matrix products, apply_taps(): jnp.einsum('oi,bihw->bohw', kernel[row_tap, col_tap], window, preferred_e...  67.6 us
    dot_general x9, matrix products, transpose_taps(): jnp.einsum('oi,bohw->bihw', kernel[row_tap, col_tap], window, preferred_e...  29.4 us
    dot_general x18, matrix products, tap_grads(): jnp.einsum('bohw,bihw->oi', upstream, window, preferred_element_type=jnp....  23.1 us
    ppermute x3, waiting for transfers between devices, with_halo(): lax.ppermute(tail, axis, [(i, (i + 1) % count) for i in range(ends)])  22.8 us
    ppermute x3, starting transfers between devices, with_halo(): lax.ppermute(tail, axis, [(i, (i + 1) % count) for i in range(ends)])  14.6 us
    unnamed x26, local copies, waits for them, and re-layouts  10.2 us
    concatenate x3, other arithmetic, with_halo(): jnp.concatenate([lax.ppermute(tail, axis, [(i, (i + 1) % count) for i in...  9.9 us
  transfers between devices with their start and end apart: 8, of which 5 were waited for; matrix products, arithmetic and copies ran while one was open for 6% of the time, Pallas kernels for 0%

commit v1 on v0

--- a/solution.py
+++ b/solution.py
@@ -127,7 +127,7 @@
     sigma = jax.nn.sigmoid(preact)
     preact_grad = (hidden_grad * (sigma * (1.0 + preact * (1.0 - sigma)))).astype(jnp.bfloat16)
     join_part = tap_grads(preact_grad, stacked_pad, tile_rows, col_count)
-    join_total, output_total = lax.psum((join_part, output_part), ("frame", "tile"))
+    join_total, output_total = lax.psum(lax.psum((join_part, output_part), "tile"), "frame")
     return (recon.astype(jnp.bfloat16), join_total, output_total)
 
 

time: 320 us -> 339 us (1.059)
  waiting for transfers between devices: 123 us -> 144 us
    psum x1 -> x2, waiting for transfers between devices: 95.2 us -> 116 us  [the longest x1 95.4 us: on_device(): lax.psum((join_part, output_part), 'tile')]
    unnamed x26 -> x28, local copies, waits for them, and re-layouts: 10.2 us -> 8.8 us
  transfers between devices with their start and end apart: 8 -> 9, of which waited for: 5 -> 6; matrix products, arithmetic and copies ran while one was open for 6% -> 5% of each run, Pallas kernels for 0% -> 0%
where the time goes in v1:
time: 339 us; the launch traced here: 336 us
  waiting for transfers between devices  144 us (42%)
  matrix products  120 us (35%)
  starting transfers between devices  19.7 us (6%)
  local copies, waits for them, and re-layouts  19.1 us (6%)
  other arithmetic  18 us (5%)
  between operations  14.7 us (4%)
    psum x1, waiting for transfers between devices, on_device(): lax.psum((join_part, output_part), 'tile')  95.4 us
    dot_general x18, matrix products, apply_taps(): jnp.einsum('oi,bihw->bohw', kernel[row_tap, col_tap], window, preferred_e...  67.4 us
    dot_general x9, matrix products, transpose_taps(): jnp.einsum('oi,bohw->bihw', kernel[row_tap, col_tap], window, preferred_e...  29.4 us
    dot_general x18, matrix products, tap_grads(): jnp.einsum('bohw,bihw->oi', upstream, window, preferred_element_type=jnp....  23.1 us
    ppermute x3, waiting for transfers between devices, with_halo(): lax.ppermute(tail, axis, [(i, (i + 1) % count) for i in range(ends)])  22.6 us
    psum x1, waiting for transfers between devices, on_device(): lax.psum(lax.psum((join_part, output_part), 'tile'), 'frame')  20.6 us
    ppermute x3, starting transfers between devices, with_halo(): lax.ppermute(tail, axis, [(i, (i + 1) % count) for i in range(ends)])  14.6 us
    concatenate x3, other arithmetic, with_halo(): jnp.concatenate([lax.ppermute(tail, axis, [(i, (i + 1) % count) for i in...  9.9 us
  transfers between devices with their start and end apart: 9, of which 6 were waited for; matrix products, arithmetic and copies ran while one was open for 5% of the time, Pallas kernels for 0%

profile of v1, /device:TPU:0, one launch (start us, length us, event | category | flops | bytes accessed | tf_op | source)
XLA Modules:
  0.0 335.6 jit_solution(13952134535757296504)
XLA Ops:
  7.2 0.8 constant_dynamic-slice_fusion
  8.0 0.9 select_reduce_fusion.1
  9.5 3.5 %gather_fusion.1 = bf16[8,96,8,256]{3,2,1,0:T(8,128)(2,1)S(1)} fusion(bf16[16,96,8,256]{3,2,1,0:T(8,128)(2,1)} %param.10, s32[1024]{0:T(1024)S(1)} %pad_clamp_fusion), kind=kCustom, calls=%fused_computation.1.clone | custom fusion | bytes 6291488 | tf_op jit(solution)/shard_map/jit(_take)/gather | solution.py:100
  13.1 2.0 select_select_fusion
  15.9 3.5 %gather_fusion = bf16[8,96,8,256]{3,2,1,0:T(8,128)(2,1)S(1)} fusion(bf16[16,96,8,256]{3,2,1,0:T(8,128)(2,1)} %param.10, s32[1024]{0:T(1024)S(1)} %pad_clamp_fusion.1), kind=kCustom, calls=%fused_computation.clone | custom fusion | bytes 6291488 | tf_op jit(solution)/shard_map/jit(_take)/gather | solution.py:105
  19.7 1.6 collective-permute-done
  21.3 2.3 select_select_fusion.1
  25.4 4.8 %collective-permute-start.1 = (bf16[4,288,1,256]{3,1,2,0:T(8,128)(2,1)S(1)}, bf16[4,288,1,256]{3,1,2,0:T(8,128)(2,1)S(1)}, u32[]{:S(2)}, u32[]{:S(2)}) collective-permute-start(bf16[4,288,1,256]{3,1,2,0:T(8,128)(2,1)S(1)} %get-tuple-element.19), channel_id=1, source_target_pairs={{0,1},{1,2},{2,3},{3,4},{4,5},{5,6},{6,7},{8,9},{9,10},{10,11},{11... | collective-permute-start | bytes 1769480 | tf_op jit(solution)/shard_map/ppermute | solution.py:19
  30.3 1.8 collective-permute-start.2
  32.0 3.0 fusion.184
  35.1 20.7 %collective-permute-done.1 = bf16[4,288,1,256]{3,1,2,0:T(8,128)(2,1)S(1)} collective-permute-done((bf16[4,288,1,256]{3,1,2,0:T(8,128)(2,1)S(1)}, bf16[4,288,1,256]{3,1,2,0:T(8,128)(2,1)S(1)}, u32[]{:S(2)}, u32[]{:S(2)}) %collective-permute-start.1) | collective-permute-done | bytes 589856 | tf_op jit(solution)/shard_map/ppermute | solution.py:19
  55.7 5.9 %fusion.5 = bf16[4,288,10,258]{3,1,2,0:T(8,128)(2,1)S(1)} fusion(bf16[4,288,1,256]{3,1,2,0:T(8,128)(2,1)S(1)} %collective-permute-done.2, bf16[4,288,8,256]{3,1,2,0:T(8,128)(2,1)S(1)} %copy_dynamic-update-slice_fusion.1, bf16[4,288,1,256]{3,1,2,0:T(8,128)(2,1)S(1)} %collective-permute-done.1), kind=kLoop, calls=%fused_computation.9 | loop fusion | flops 35665920 | bytes 11842560 | tf_op jit(solution)/shard_map/concatenate | solution.py:17
  61.7 3.0 fusion.13
  64.7 3.3 fusion.17
  68.0 3.0 fusion.21
  70.9 3.3 fusion.25
  74.2 3.0 fusion.29
  77.2 3.0 fusion.44
  80.2 3.0 fusion.42
  83.2 11.2 %fusion.38 = (bf16[4,96,8,256]{3,1,2,0:T(8,128)(2,1)}, f32[4,8,256,96]{2,3,1,0:T(8,128)}) fusion(bf16[4,288,10,258]{3,1,2,0:T(8,128)(2,1)S(1)} %fusion.5, bf16[3,3,96,288]{3,2,1,0:T(8,128)(2,1)} %param.16, f32[4,8,256,96]{2,3,1,0:T(8,128)} %fusion.44, f32[4,8,256,96]{2,3,1,0:T(8,128)} %fusion.13, f32[4,8,256,96]{2,3,1,0:T(8,128)} %fusion.17, ...), kind=kOutput, calls=%fused_computation.52 | convolution fusion | flops 463208448 | bytes 34676736 | tf_op jit(solution)/shard_map/oi,bihw->bohw/dot_general | solution.py:37
  94.3 1.2 fusion.249
  95.5 4.4 %collective-permute-start.3 = (bf16[4,96,1,256]{3,1,2,0:T(8,128)(2,1)S(1)}, bf16[4,96,1,256]{3,1,2,0:T(8,128)(2,1)S(1)}, u32[]{:S(2)}, u32[]{:S(2)}) collective-permute-start(bf16[4,96,1,256]{3,1,2,0:T(8,128)(2,1)S(1)} %get-tuple-element.23), channel_id=1, source_target_pairs={{0,1},{1,2},{2,3},{3,4},{4,5},{5,6},{6,7},{8,9},{9,10},{10,11},{11... | collective-permute-start | bytes 589832 | tf_op jit(solution)/shard_map/ppermute | solution.py:19
  99.9 1.5 collective-permute-start.4
  101.4 3.7 %fusion.209 = f32[4,8,256,96]{2,3,1,0:T(8,128)} fusion(bf16[4,96,8,256]{3,1,2,0:T(8,128)(2,1)} %get-tuple-element.27, bf16[3,3,96,96]{3,2,1,0:T(8,128)(2,1)S(1)} %copy-done.5), kind=kOutput, calls=%fused_computation.183 | convolution fusion | flops 150994944 | bytes 4743168 | tf_op jit(solution)/shard_map/oi,bihw->bohw/dot_general | solution.py:37
  105.1 3.9 %collective-permute-done.4 = bf16[4,96,1,256]{3,1,2,0:T(8,128)(2,1)S(1)} collective-permute-done((bf16[4,96,1,256]{3,1,2,0:T(8,128)(2,1)S(1)}, bf16[4,96,1,256]{3,1,2,0:T(8,128)(2,1)S(1)}, u32[]{:S(2)}, u32[]{:S(2)}) %collective-permute-start.4) | collective-permute-done | bytes 196640 | tf_op jit(solution)/shard_map/ppermute | solution.py:21
  109.0 2.0 select_maximum_fusion.2
  111.0 2.2 fusion.76
  113.2 2.3 fusion.80
  115.6 2.2 fusion.84
  117.8 2.3 fusion.88
  120.1 2.2 fusion.92
  122.3 2.3 fusion.175
  124.6 2.3 fusion.174
  126.9 12.3 %bitcast_convert_fusion = (bf16[4,96,8,256]{3,1,2,0:T(8,128)(2,1)}, f32[4,8,256,96]{2,3,1,0:T(8,128)}) fusion(bf16[4,96,10,258]{3,1,2,0:T(8,128)(2,1)S(1)} %select_maximum_fusion.2, bf16[3,3,96,96]{3,2,1,0:T(8,128)(2,1)S(1)} %copy-done.5, f32[4,8,256,96]{2,3,1,0:T(8,128)} %fusion.175, f32[4,8,256,96]{2,3,1,0:T(8,128)} %fusion.76, ...), kind=kOutput, calls=%fused_computation.42 | convolution fusion | flops 158072832 | bytes 31481856 | tf_op jit(solution)/shard_map/oi,bihw->bohw/dot_general | solution.py:37
  139.1 2.6 fusion.34
  142.3 2.3 fusion.207
  144.6 1.3 collective-permute-start.6
  145.9 5.4 %collective-permute-start.5 = (bf16[4,96,1,256]{3,1,2,0:T(8,128)(2,1)S(1)}, bf16[4,96,1,256]{3,1,2,0:T(8,128)(2,1)S(1)}, u32[]{:S(2)}, u32[]{:S(2)}) collective-permute-start(bf16[4,96,1,256]{3,1,2,0:T(8,128)(2,1)S(1)} %get-tuple-element.22), channel_id=1, source_target_pairs={{0,1},{1,2},{2,3},{3,4},{4,5},{5,6},{6,7},{8,9},{9,10},{10,11},{11... | collective-permute-start | bytes 589832 | tf_op jit(solution)/shard_map/ppermute | solution.py:19
  151.9 0.8 fusion.144
  156.5 1.9 collective-permute-done.5
  158.5 2.0 select_maximum_fusion
  160.5 2.4 fusion.58
  162.9 2.3 fusion.60
  165.2 2.4 fusion.62
  167.6 2.3 fusion.64
  169.9 2.5 fusion.66
  172.4 2.3 fusion.50
  174.6 2.3 fusion.46
  176.9 10.6 %fusion.31 = bf16[4,96,8,256]{3,1,2,0:T(8,128)(2,1)S(1)} fusion(f32[4,8,256,96]{2,3,1,0:T(8,128)} %get-tuple-element.28, f32[4,8,256,96]{2,3,1,0:T(8,128)} %fusion.50, f32[4,8,256,96]{2,3,1,0:T(8,128)} %fusion.58, f32[4,8,256,96]{2,3,1,0:T(8,128)} %fusion.60, f32[4,8,256,96]{2,3,1,0:T(8,128)} %fusion.207, f32[4,8,256,96]{2,3,1,0:T(8,128)} %fusion.62, ...), kind=kOutput, calls=%fused_computation.40 | convolution fusion | flops 164364288 | bytes 31481856 | tf_op jit(solution)/shard_map/oi,bohw->bihw/dot_general | solution.py:66
  187.6 1.8 fusion.101
  189.3 1.8 fusion.97
  191.1 2.3 fusion.107
  193.4 1.8 fusion.113
  195.2 1.8 fusion.134
  196.9 2.3 fusion.119
  199.2 1.8 fusion.125
  201.0 1.8 fusion.95
  202.8 2.3 fusion.131
  205.1 1.1 copy-done.4
  206.2 95.4 %all-reduce.8.cloned.1.call-done = (f32[3,3,96,288]{3,2,1,0:T(8,128)}, f32[3,3,96,96]{3,2,1,0:T(8,128)}) async-done(((f32[3,3,96,288]{3,2,1,0:T(8,128)}, f32[3,3,96,96]{3,2,1,0:T(8,128)}), (f32[3,3,96,288]{3,2,1,0:T(8,128)}, f32[3,3,96,96]{3,2,1,0:T(8,128)})) %all-reduce.8.cloned.1.call-update) | async-done | bytes 1327120 | tf_op jit(solution)/shard_map/psum | solution.py:130
  301.6 2.0 copy.56
  303.6 20.6 %all-reduce.10.cloned.1.call-done = (f32[3,3,96,288]{3,2,1,0:T(8,128)}, f32[3,3,96,96]{3,2,1,0:T(8,128)}) async-done(((f32[3,3,96,288]{3,2,1,0:T(8,128)}, f32[3,3,96,96]{3,2,1,0:T(8,128)}), (f32[3,3,96,288]{3,2,1,0:T(8,128)}, f32[3,3,96,96]{3,2,1,0:T(8,128)})) %all-reduce.10.cloned.1.call-update) | async-done | bytes 1327120 | tf_op jit(solution)/shard_map/psum | solution.py:130
  324.2 2.5 copy.135
  326.7 1.8 copy.136
  (62 shorter events, 8.5 us)
Async XLA Ops:
  7.2 294.4 %all-reduce.8.cloned.1.call-start = ((), (), s32[]{:S(2)}) async-start(), calls=%async_computation | async-start | bytes 3538944 | tf_op jit(solution)/shard_map/psum | solution.py:130
  13.1 2.6 copy-start.10
  15.1 6.1 %collective-permute-start = (bf16[8,96,8,256]{3,2,1,0:T(8,128)(2,1)}, bf16[8,96,8,256]{3,2,1,0:T(8,128)(2,1)}, u32[]{:S(2)}, u32[]{:S(2)}) collective-permute-start(bf16[8,96,8,256]{3,2,1,0:T(8,128)(2,1)} %select_select_fusion), channel_id=1, source_target_pairs={{0,8},{8,0},{1,9},{9,1},{2,10},{10,2},{3,11},{11,3},{4,12},{12,4},... | collective-permute-start | bytes 9437192 | tf_op jit(solution)/shard_map/ppermute | solution.py:8
  15.9 3.6 %copy-start.11 = (f32[32]{0:T(128)S(1)}, f32[32]{0:T(128)}, u32[]{:S(2)}) copy-start(f32[32]{0:T(128)} %param.15) | copy-start | bytes 388
  23.6 1.4 copy-start.2
  25.0 7.0 %copy-start.9 = (bf16[3,3,96,288]{3,2,1,0:T(8,128)(2,1)S(1)}, bf16[3,3,96,288]{3,2,1,0:T(8,128)(2,1)}, u32[]{:S(2)}) copy-start(bf16[3,3,96,288]{3,2,1,0:T(8,128)(2,1)} %param.16) | copy-start | bytes 1492996
  25.4 30.3 %collective-permute-start.1 = (bf16[4,288,1,256]{3,1,2,0:T(8,128)(2,1)S(1)}, bf16[4,288,1,256]{3,1,2,0:T(8,128)(2,1)S(1)}, u32[]{:S(2)}, u32[]{:S(2)}) collective-permute-start(bf16[4,288,1,256]{3,1,2,0:T(8,128)(2,1)S(1)} %get-tuple-element.19), channel_id=1, source_target_pairs={{0,1},{1,2},{2,3},{3,4},{4,5},{5,6},{6,7},{8,9},{9,10},{10,11},{11... | collective-permute-start | bytes 1769480 | tf_op jit(solution)/shard_map/ppermute | solution.py:19
  30.3 25.5 %collective-permute-start.2 = (bf16[4,288,1,256]{3,1,2,0:T(8,128)(2,1)S(1)}, bf16[4,288,1,256]{3,1,2,0:T(8,128)(2,1)S(1)}, u32[]{:S(2)}, u32[]{:S(2)}) collective-permute-start(bf16[4,288,1,256]{3,1,2,0:T(8,128)(2,1)S(1)} %get-tuple-element.20), channel_id=1, source_target_pairs={{1,0},{2,1},{3,2},{4,3},{5,4},{6,5},{7,6},{9,8},{10,9},{11,10},{12... | collective-permute-start | bytes 1769480 | tf_op jit(solution)/shard_map/ppermute | solution.py:21
  55.7 24.4 %copy-start.6 = (bf16[4,288,1,256]{3,1,2,0:T(8,128)(2,1)}, bf16[4,288,1,256]{3,1,2,0:T(8,128)(2,1)S(1)}, u32[]{:S(2)}) copy-start(bf16[4,288,1,256]{3,1,2,0:T(8,128)(2,1)S(1)} %collective-permute-done.1) | copy-start | bytes 1769476
  83.2 18.2 %copy-start.5 = (bf16[3,3,96,96]{3,2,1,0:T(8,128)(2,1)S(1)}, bf16[3,3,96,96]{3,2,1,0:T(8,128)(2,1)}, u32[]{:S(2)}) copy-start(bf16[3,3,96,96]{3,2,1,0:T(8,128)(2,1)} %param.17) | copy-start | bytes 497668
  94.3 14.7 %copy-start = (bf16[4,96,8,256]{3,1,2,0:T(8,128)(2,1)S(1)}, bf16[4,96,8,256]{3,1,2,0:T(8,128)(2,1)}, u32[]{:S(2)}) copy-start(bf16[4,96,8,256]{3,1,2,0:T(8,128)(2,1)} %get-tuple-element.27) | copy-start | bytes 4718596
  95.5 9.6 %collective-permute-start.3 = (bf16[4,96,1,256]{3,1,2,0:T(8,128)(2,1)S(1)}, bf16[4,96,1,256]{3,1,2,0:T(8,128)(2,1)S(1)}, u32[]{:S(2)}, u32[]{:S(2)}) collective-permute-start(bf16[4,96,1,256]{3,1,2,0:T(8,128)(2,1)S(1)} %get-tuple-element.23), channel_id=1, source_target_pairs={{0,1},{1,2},{2,3},{3,4},{4,5},{5,6},{6,7},{8,9},{9,10},{10,11},{11... | collective-permute-start | bytes 589832 | tf_op jit(solution)/shard_map/ppermute | solution.py:19
  99.9 9.1 %collective-permute-start.4 = (bf16[4,96,1,256]{3,1,2,0:T(8,128)(2,1)S(1)}, bf16[4,96,1,256]{3,1,2,0:T(8,128)(2,1)S(1)}, u32[]{:S(2)}, u32[]{:S(2)}) collective-permute-start(bf16[4,96,1,256]{3,1,2,0:T(8,128)(2,1)S(1)} %get-tuple-element.24), channel_id=1, source_target_pairs={{1,0},{2,1},{3,2},{4,3},{5,4},{6,5},{7,6},{9,8},{10,9},{11,10},{12... | collective-permute-start | bytes 589832 | tf_op jit(solution)/shard_map/ppermute | solution.py:21
  126.9 12.3 %copy-start.3 = (bf16[4,96,8,256]{3,2,1,0:T(8,128)(2,1)S(1)}, bf16[4,96,8,256]{3,2,1,0:T(8,128)(2,1)}, u32[]{:S(2)}) copy-start(bf16[4,96,8,256]{3,2,1,0:T(8,128)(2,1)} %param.11) | copy-start | bytes 4718596
  144.6 11.9 %collective-permute-start.6 = (bf16[4,96,1,256]{3,1,2,0:T(8,128)(2,1)S(1)}, bf16[4,96,1,256]{3,1,2,0:T(8,128)(2,1)S(1)}, u32[]{:S(2)}, u32[]{:S(2)}) collective-permute-start(bf16[4,96,1,256]{3,1,2,0:T(8,128)(2,1)S(1)} %get-tuple-element.21), channel_id=1, source_target_pairs={{1,0},{2,1},{3,2},{4,3},{5,4},{6,5},{7,6},{9,8},{10,9},{11,10},{12... | collective-permute-start | bytes 589832 | tf_op jit(solution)/shard_map/ppermute | solution.py:21
  145.9 12.6 %collective-permute-start.5 = (bf16[4,96,1,256]{3,1,2,0:T(8,128)(2,1)S(1)}, bf16[4,96,1,256]{3,1,2,0:T(8,128)(2,1)S(1)}, u32[]{:S(2)}, u32[]{:S(2)}) collective-permute-start(bf16[4,96,1,256]{3,1,2,0:T(8,128)(2,1)S(1)} %get-tuple-element.22), channel_id=1, source_target_pairs={{0,1},{1,2},{2,3},{3,4},{4,5},{5,6},{6,7},{8,9},{9,10},{10,11},{11... | collective-permute-start | bytes 589832 | tf_op jit(solution)/shard_map/ppermute | solution.py:19
  156.5 6.4 %copy-start.8 = (f32[9,96,96]{2,1,0:T(8,128)}, f32[9,96,96]{2,1,0:T(8,128)S(1)}, u32[]{:S(2)}) copy-start(f32[9,96,96]{2,1,0:T(8,128)S(1)} %fusion.168) | copy-start | bytes 995332
  187.6 1.8 copy-start.7
  205.0 1.1 copy-start.4
  206.1 95.5 %copy-start.1 = (bf16[4,96,8,256]{3,1,2,0:T(8,128)(2,1)S(1)}, bf16[4,96,8,256]{3,1,2,0:T(8,128)(2,1)}, u32[]{:S(2)}) copy-start(bf16[4,96,8,256]{3,1,2,0:T(8,128)(2,1)} %get-tuple-element.29) | copy-start | bytes 4718596
  206.1 118.1 %all-reduce.10.cloned.1.call-start = ((), (), s32[]{:S(2)}) async-start(), calls=%async_computation.1 | async-start | bytes 3538944 | tf_op jit(solution)/shard_map/psum | solution.py:130
Sparse Core Ops, SparseCore 0:
  206.3 95.2 all-reduce.7
  304.0 20.1 all-reduce.9
